TPU v7x, 32 devices: a whole 2x2x4 slice. The times are simulated.
32 devices in a mesh: groups: 2 (over x), seq: 16 (over z, y, core).
Axes of the slice: x: 2, y: 2, z: 4, core: 2. Of those that a mesh axis runs over, the one named last changes fastest.
Arguments:
- queries: bfloat16 [32, 8192], P(('groups', 'seq')), parts along dimension 0, may hold values from -320 to 320, as said below
- span_keys: bfloat16 [32, 1024], P(('groups', 'seq')), parts along dimension 0, may hold values from -6 to 6
- span_values: bfloat16 [32, 1024], P(('groups', 'seq')), parts along dimension 0, may hold values from -6 to 6
- cache_keys: bfloat16 [8192, 1024], P(('groups', 'seq')), parts along dimension 0, may hold values from -6 to 6
- cache_values: bfloat16 [8192, 1024], P(('groups', 'seq')), parts along dimension 0, may hold values from -6 to 6
- page_table: int32 [512], P(('groups', 'seq')), parts along dimension 0, may hold values from 0 to 255, each once
- page_counts: int32 [32], P(('groups', 'seq')), parts along dimension 0, may hold values from 1 to 16, 128 in all
- span_start: int32 [2], P('groups'), parts along dimension 0, may hold values from 2048 to 4095
Outputs:
- attended: bfloat16 [32, 8192], P(('groups', 'seq')), parts along dimension 0
There are 2 independent parts, one for each index of `groups`. A program takes and returns all parts, laid end to end along the dimension named above; each array names one. Nothing has to cross between parts.
Inputs may be any that keep to these rules, and one draw needn't show every extreme that they name: `queries`: queries of every row; in some draws rows differ in scale by a large factor. `page_table`: A permutation of the 256 logical pages. `page_counts`: counts of the shards sum to 128; slots at or beyond a shard's count hold no page; some shard holds 16.
All inputs are finite; a program needn't handle non-finite values.
Results may differ from a plain program's by a relative error of at most 0.02.
The roundings to bfloat16 on the way count: a program that leaves them out, or rounds other values in their place, can miss the bound.
Values may be sent and summed in bfloat16 or wider, within the bound.
A program may use at most 64 MiB of HBM per device.

v0:
```python
import functools
import math

import jax
import jax.numpy as jnp
import numpy as np
from jax import lax
from jax.experimental import pallas as pl
from jax.experimental.pallas import tpu as pltpu
from jax.sharding import PartitionSpec as P

H = 64
KVH = 8
PAGE = 16
GROUP = H // KVH
HALF_KV = KVH // 2
HALF_H = H // 2
SPAN_PAD = 16

rope_base = 1000000.0
masked_low = -1e30
no_page = float(1 << 20)
MESH = pl.DeviceIdType.MESH


def angle_table(width):
    half = width // 2
    turns = rope_base ** (-(np.arange(half) * 2.0 / width)) / (2.0 * math.pi)
    mant, expo = np.frexp(turns)
    high = np.ldexp(np.floor(mant * 4096.0) / 4096.0, expo)
    rows = np.zeros((8, width), np.float32)
    rows[0] = np.tile(high, 2)
    rows[1] = np.tile(turns - high, 2)
    rows[2] = np.tile(turns, 2)
    rows[3, :half] = 0.25
    return rows


def cos_sin(high_pos, low_pos, tab):
    x = high_pos * tab[0:1]
    x = x - jnp.floor(x + 0.5)
    x = x + (high_pos * tab[1:2] + (low_pos * tab[2:3] + tab[3:4]))
    x = x - jnp.floor(x + 0.5)
    y = jnp.where(x > 0.25, 0.5 - x, jnp.where(x < -0.25, -0.5 - x, x))
    z = y * (2.0 * math.pi)
    z2 = z * z
    acc = jnp.full_like(z2, 1.0 / math.factorial(13))
    for order, sign in ((11, -1.0), (9, 1.0), (7, -1.0), (5, 1.0), (3, -1.0), (1, 1.0)):
        acc = acc * z2 + sign / math.factorial(order)
    both = acc * z
    half = both.shape[-1] // 2
    turned = pltpu.roll(both, half, both.ndim - 1)
    low = lax.broadcasted_iota(jnp.int32, both.shape, both.ndim - 1) < half
    return jnp.where(low, both, turned), jnp.where(low, -turned, both)


def rotate(x, cosine, sine):
    return x * cosine + pltpu.roll(x, x.shape[-1] // 2, x.ndim - 1) * sine


def kernel(
    n, factor,
    table_hbm, counts_hbm, start_hbm,
    q_hbm, sk_hbm, sv_hbm, tab_hbm, keys_hbm, vals_hbm,
    out_ref,
    table_ref, counts_ref, start_ref,
    q_in, sk_in, sv_in, tab_in, keys_raw, vals, keys_rot,
    q_own, q_all, page_own, page_peer, span_own, span_peer,
    num_send, stat_send, num_recv, stat_recv,
    in_sem, peer_send, peer_recv, q_send, q_recv, num_ss, num_rs, stat_ss, stat_rs,
):
    me = lax.axis_index("seq")
    core = lax.rem(me, 2)
    partner = me + 1 - 2 * core
    rows = keys_hbm.shape[0]
    width = tab_hbm.shape[1]
    slots = rows // PAGE
    cols = HALF_KV * width
    chips = n // 2
    unroll = n <= 16 and n & (n - 1) == 0

    def flipped(i):
        peer, bit = me, 1
        while bit < n:
            if i & bit:
                peer = peer + bit * (1 - 2 * lax.rem(me // bit, 2))
            bit *= 2
        return peer

    def forward(i):
        return flipped(i) if unroll else lax.rem(me + i, n)

    def backward(i):
        return flipped(i) if unroll else lax.rem(me + n - i, n)

    def steps(low, high, step):
        if unroll:
            for i in reversed(range(low, high)):
                step(i)
        else:
            def one(i, carry):
                step(i)
                return carry
            lax.fori_loop(low, high, one, 0)

    barrier = pltpu.get_barrier_semaphore()

    def greet(i):
        pl.semaphore_signal(
            barrier, inc=1, device_id={"seq": forward(i)}, device_id_type=MESH
        )

    steps(1, n, greet)

    small = [
        pltpu.make_async_copy(src, dst, in_sem.at[i])
        for i, (src, dst) in enumerate(
            (
                (start_hbm, start_ref), (q_hbm, q_in), (tab_hbm, tab_in), (sk_hbm, sk_in),
                (sv_hbm, sv_in), (table_hbm, table_ref), (counts_hbm, counts_ref),
            )
        )
    ]
    for copy in small:
        copy.start()
    mine = pl.ds(pl.multiple_of(core * cols, cols), cols)
    theirs = pl.ds(pl.multiple_of((1 - core) * cols, cols), cols)
    own_keys = pltpu.make_async_copy(
        keys_hbm.at[:, mine], keys_raw.at[pl.ds(0, rows), :], in_sem.at[7]
    )
    own_vals = pltpu.make_async_copy(
        vals_hbm.at[:, mine], vals.at[pl.ds(0, rows), :], in_sem.at[8]
    )
    own_keys.start()
    own_vals.start()

    def by_head(ref, heads):
        row = ref[...].astype(jnp.float32)
        return jnp.concatenate(
            [row[:, h * width : (h + 1) * width] for h in range(heads)], axis=0
        )

    for copy in small:
        copy.wait()
    start = start_ref[0]
    tab = tab_in[...]
    here = start + me
    high = (here // PAGE) * PAGE
    cosine, sine = cos_sin(
        jnp.full((8, width), high.astype(jnp.float32)),
        jnp.full((8, width), (here - high).astype(jnp.float32)),
        tab,
    )
    cosine, sine = cosine[0:1], sine[0:1]
    q_rot = rotate(by_head(q_in, H), cosine, sine).astype(jnp.bfloat16)
    q_own[...] = q_rot.reshape(2, HALF_H, width)
    k_rot = rotate(by_head(sk_in, KVH), cosine, sine)
    v_own = by_head(sv_in, KVH)
    for half in range(2):
        part = slice(half * HALF_KV, (half + 1) * HALF_KV)
        span_own[half] = jnp.concatenate([k_rot[part], v_own[part]], axis=0)
    slot = lax.broadcasted_iota(jnp.int32, (slots, width), 0)
    pages = jnp.zeros((slots, width), jnp.float32)
    for j in range(slots):
        pages = jnp.where(slot == j, (table_ref[j] * PAGE).astype(jnp.float32), pages)
    pages = jnp.where(slot < counts_ref[0], pages, no_page)
    page_own[...] = pages

    pl.semaphore_wait(barrier, n - 1)

    def q_copy(i):
        peer = forward(i)
        return pltpu.make_async_remote_copy(
            src_ref=q_own.at[lax.rem(peer, 2)], dst_ref=q_all.at[i],
            send_sem=q_send.at[0], recv_sem=q_recv.at[0],
            device_id={"seq": peer}, device_id_type=MESH,
        )

    steps(1, n, lambda i: q_copy(i).start())

    def wait_all(ref, send_sem, recv_sem):
        rest = ref.at[pl.ds(1, n - 1)]
        pltpu.make_async_remote_copy(
            src_ref=rest, dst_ref=rest, send_sem=send_sem.at[0], recv_sem=recv_sem.at[0],
            device_id={"seq": partner}, device_id_type=MESH,
        ).wait()

    def to_partner(src, dst, i):
        return pltpu.make_async_remote_copy(
            src_ref=src, dst_ref=dst, send_sem=peer_send.at[i], recv_sem=peer_recv.at[i],
            device_id={"seq": partner}, device_id_type=MESH,
        )

    other = pl.ds(rows, rows)
    exchange = [
        to_partner(page_own, page_peer, 0),
        to_partner(span_own.at[1 - core], span_peer, 1),
        to_partner(keys_hbm.at[:, theirs], keys_raw.at[other, :], 2),
        to_partner(vals_hbm.at[:, theirs], vals.at[other, :], 3),
    ]
    for copy in exchange:
        copy.start()
    q_all[0] = q_own[core]

    def fill_keys(page_values, base):
        in_page = lax.broadcasted_iota(jnp.int32, (PAGE, width), 0).astype(jnp.float32)
        for j in range(slots):
            at = pl.ds(base + j * PAGE, PAGE)
            c, s = cos_sin(
                jnp.broadcast_to(page_values[j : j + 1], (PAGE, width)), in_page, tab
            )
            for k in range(HALF_KV):
                x = keys_raw[at, k * width : (k + 1) * width].astype(jnp.float32)
                keys_rot[k, at, :] = rotate(x, c, s).astype(jnp.bfloat16)

    def live_bias(page_values):
        wide = jnp.concatenate([page_values] * (rows // width), axis=1)
        lane = lax.broadcasted_iota(jnp.int32, (slots, rows), 1)
        row = lax.broadcasted_iota(jnp.int32, (slots, rows), 0)
        picked = jnp.sum(jnp.where(lane // PAGE == row, wide, 0.0), axis=0, keepdims=True)
        position = picked + lax.rem(lane[0:1], PAGE).astype(jnp.float32)
        return jnp.where(position < start.astype(jnp.float32), 0.0, masked_low)

    own_keys.wait()
    fill_keys(pages, 0)
    bias_own = live_bias(pages)
    own_vals.wait()
    exchange[0].wait()
    exchange[1].wait()
    mine_span = span_own[core]
    peer_span = span_peer[...]
    line = lax.broadcasted_iota(jnp.int32, (SPAN_PAD, width), 0)
    for k in range(HALF_KV):
        for buffer, r in ((0, k), (1, HALF_KV + k)):
            block = jnp.where(
                line == 0, mine_span[r : r + 1],
                jnp.where(line == 1, peer_span[r : r + 1], 0.0),
            ).astype(jnp.bfloat16)
            if buffer == 0:
                keys_rot[k, pl.ds(2 * rows, SPAN_PAD), :] = block
            else:
                vals[pl.ds(2 * rows, SPAN_PAD), k * width : (k + 1) * width] = block
    pages_peer = page_peer[...]
    bias_peer = live_bias(pages_peer)
    exchange[2].wait()
    fill_keys(pages_peer, rows)
    exchange[3].wait()

    bias = jnp.concatenate([bias_own, bias_peer], axis=1)
    count = n
    row_count = count * GROUP
    column = lax.broadcasted_iota(jnp.int32, (row_count, SPAN_PAD), 1)
    lane = lax.broadcasted_iota(jnp.int32, (row_count, width), 1)
    member = lax.rem(lax.broadcasted_iota(jnp.int32, (row_count, width), 0), GROUP)
    own_lane = lax.rem(lane, GROUP) == member
    lane_head = lane // GROUP

    def place(i):
        return lax.rem(i, 2) * chips + i // 2

    def num_copy(i):
        return pltpu.make_async_remote_copy(
            src_ref=num_send.at[i], dst_ref=num_recv.at[place(i)],
            send_sem=num_ss.at[0], recv_sem=num_rs.at[0],
            device_id={"seq": backward(i)}, device_id_type=MESH,
        )

    def stat_copy(i):
        return pltpu.make_async_remote_copy(
            src_ref=stat_send.at[i], dst_ref=stat_recv.at[place(i)],
            send_sem=stat_ss.at[0], recv_sem=stat_rs.at[0],
            device_id={"seq": backward(i)}, device_id_type=MESH,
        )

    def serve(first):
        these = pl.ds(first, count)
        wait_all(q_all, q_send, q_recv)
        token = jnp.concatenate(
            [jnp.full((GROUP, SPAN_PAD), backward(first + i), jnp.int32) for i in range(count)],
            axis=0,
        )
        seen = ((column == 0) & (token >= me)) | ((column == 1) & (token >= partner))
        span_bias = jnp.where(seen, 0.0, masked_low)
        stats = jnp.zeros((row_count, width), jnp.float32)
        for pair in range(HALF_KV // 2):
            both = pl.ds(pair * 2 * GROUP, 2 * GROUP)
            q_pair = q_all[these, both, :].astype(jnp.float32)
            numer = []
            for side in range(2):
                k = pair * 2 + side
                q_one = q_pair[:, side * GROUP : (side + 1) * GROUP, :]
                q_one = q_one.reshape(row_count, width).astype(jnp.bfloat16)
                scores = lax.dot_general(
                    q_one, keys_rot[k, pl.ds(0, 2 * rows), :], (((1,), (1,)), ((), ())),
                    preferred_element_type=jnp.float32,
                ) + bias
                near = lax.dot_general(
                    q_one, keys_rot[k, pl.ds(2 * rows, SPAN_PAD), :], (((1,), (1,)), ((), ())),
                    preferred_element_type=jnp.float32,
                ) + span_bias
                best = jnp.maximum(
                    jnp.max(scores, axis=1, keepdims=True), jnp.max(near, axis=1, keepdims=True)
                )
                w = jnp.exp((scores - best) * factor)
                w_near = jnp.exp((near - best) * factor)
                den = jnp.sum(w, axis=1, keepdims=True) + jnp.sum(w_near, axis=1, keepdims=True)
                at = slice(k * width, (k + 1) * width)
                num = jnp.dot(
                    w.astype(jnp.bfloat16), vals[pl.ds(0, 2 * rows), at],
                    preferred_element_type=jnp.float32,
                ) + jnp.dot(
                    w_near.astype(jnp.bfloat16), vals[pl.ds(2 * rows, SPAN_PAD), at],
                    preferred_element_type=jnp.float32,
                )
                numer.append(num.reshape(count, GROUP, width))
                stats = jnp.where(lane_head == k, best, stats)
                stats = jnp.where(lane_head == HALF_KV + k, den, stats)
            num_send[these, both, :] = jnp.concatenate(numer, axis=1).astype(jnp.bfloat16)
            if pair == HALF_KV // 2 - 1:
                kept = jnp.where(own_lane, stats, 0.0).reshape(count, GROUP, width)
                stat_send[these] = jnp.sum(kept, axis=1, keepdims=True)

    serve(0)

    def answer(i):
        stat_copy(i).start()
        num_copy(i).start()

    steps(1, n, answer)
    num_recv[0] = num_send[0]
    stat_recv[0] = stat_send[0]

    wait_all(stat_recv, stat_ss, stat_rs)
    got = stat_recv[...].reshape(n, width)
    parts = []
    for half in range(2):
        r = got[half * chips : (half + 1) * chips]
        e = jnp.exp((r - jnp.max(r, axis=0, keepdims=True)) * factor)
        d = pltpu.roll(r, width - HALF_H, 1)
        total = jnp.sum(e * d, axis=0, keepdims=True)
        valid = lax.broadcasted_iota(jnp.int32, total.shape, 1) < HALF_H
        parts.append(e / jnp.where(valid, total, 1.0))
    weights = jnp.concatenate(parts, axis=0).T
    pieces = [[], []]
    wait_all(num_recv, num_ss, num_rs)
    for pair in range(HALF_KV // 2):
        both = slice(pair * 2 * GROUP, (pair + 1) * 2 * GROUP)
        acc = [jnp.zeros((2 * GROUP, width), jnp.float32)] * 2
        for i in range(n):
            half = i % 2
            s = half * chips + i // 2
            acc[half] = acc[half] + weights[both, s : s + 1] * num_recv[s, both, :].astype(
                jnp.float32
            )
        for half in range(2):
            pieces[half].append(acc[half])
    same, swapped = (jnp.concatenate(p, axis=0) for p in pieces)
    for half in range(2):
        block = jnp.where(core == half, same, swapped).astype(jnp.bfloat16)
        for h in range(HALF_H):
            at = (half * HALF_H + h) * width
            out_ref[:, at : at + width] = block[h : h + 1]


def body(
    n, queries, span_keys, span_values, cache_keys, cache_values, page_table, page_counts, span_start
):
    assert queries.shape[0] == 1 and n % 2 == 0
    width = queries.shape[1] // H
    rows = cache_keys.shape[0]
    cols = HALF_KV * width
    bf16, f32, i32 = jnp.bfloat16, jnp.float32, jnp.int32
    dma = pltpu.SemaphoreType.DMA
    total = 2 * rows + SPAN_PAD
    return pl.pallas_call(
        functools.partial(kernel, n, width ** (-0.5)),
        out_shape=jax.ShapeDtypeStruct((1, H * width), bf16),
        in_specs=[pl.BlockSpec(memory_space=pltpu.HBM)] * 9,
        out_specs=pl.BlockSpec(memory_space=pltpu.VMEM),
        scratch_shapes=[
            pltpu.SMEM(page_table.shape, i32),
            pltpu.SMEM((1,), i32),
            pltpu.SMEM((1,), i32),
            pltpu.VMEM((1, H * width), bf16),
            pltpu.VMEM((1, KVH * width), bf16),
            pltpu.VMEM((1, KVH * width), bf16),
            pltpu.VMEM((8, width), f32),
            pltpu.VMEM((2 * rows, cols), bf16),
            pltpu.VMEM((total, cols), bf16),
            pltpu.VMEM((HALF_KV, total, width), bf16),
            pltpu.VMEM((2, HALF_H, width), bf16),
            pltpu.VMEM((n, HALF_H, width), bf16),
            pltpu.VMEM((rows // PAGE, width), f32),
            pltpu.VMEM((rows // PAGE, width), f32),
            pltpu.VMEM((2, 2 * HALF_KV, width), f32),
            pltpu.VMEM((2 * HALF_KV, width), f32),
            pltpu.VMEM((n, HALF_H, width), bf16),
            pltpu.VMEM((n, 1, width), f32),
            pltpu.VMEM((n, HALF_H, width), bf16),
            pltpu.VMEM((n, 1, width), f32),
            dma((9,)), dma((4,)), dma((4,)),
            dma((1,)), dma((1,)), dma((1,)), dma((1,)), dma((1,)), dma((1,)),
        ],
        compiler_params=pltpu.CompilerParams(collective_id=0, has_side_effects=True),
    )(
        page_table, page_counts, span_start, queries, span_keys, span_values,
        jnp.asarray(angle_table(width)), cache_keys, cache_values,
    )


def solution(mesh):
    in_specs = (
        P(("groups", "seq"), None),
        P(("groups", "seq"), None),
        P(("groups", "seq"), None),
        P(("groups", "seq"), None),
        P(("groups", "seq"), None),
        P(("groups", "seq")),
        P(("groups", "seq")),
        P("groups"),
    )
    out_specs = P(("groups", "seq"), None)
    return jax.shard_map(
        functools.partial(body, mesh.shape["seq"]), mesh=mesh, in_specs=in_specs,
        out_specs=out_specs, check_vma=False,
    )
```

profile of v0, /device:TPU:0, one launch (start us, length us, event | category | flops | bytes accessed | tf_op | source)
XLA Modules:
  0.0 20.6 jit_solution(7226094621606801139)
XLA Ops:
  1.3 17.9 %shard_map.91 = bf16[1,8192]{1,0:T(2,128)(2,1)} custom-call(s32[16]{0:T(128)} %table_hbm.1, s32[1]{0:T(128)S(6)} %copy.11.counts_hbm, s32[1]{0:T(128)S(6)} %copy.12.start_hbm, bf16[1,8192]{1,0:T(2,128)(2,1)} %q_hbm.1, bf16[1,1024]{1,0:T(2,128)(2,1)} %sk_hbm.1, bf16[1,1024]{1,0:T(2,128)(2,1)} %sv_hbm.1, f32[8,128]{1,0:T(8,128)} %constant.2.clone.tab_hbm, ...), custom_call_target="tpu_custom_call" | custom-call | tf_op jit(solution)/shard_map/pallas_call | solution.py:375
  19.2 1.4 %copy.13 = bf16[1,8192]{1,0:T(2,128)(2,1)} copy(bf16[1,8192]{1,0:T(2,128)(2,1)} %shard_map.91) | data formatting | bytes 32768
where the time goes:
time: 20.8 us; the launch traced here: 20.6 us
  Pallas kernels  17.9 us (86%)
  local copies, waits for them, and re-layouts  1.41 us (7%)
  between operations  1.3 us (6%)
    pallas_call x1, Pallas kernels, body(): pl.pallas_call(functools.partial(kernel, n, width ** (-0.5)), out_shape=j...  17.9 us
    unnamed x1, local copies, waits for them, and re-layouts  1.41 us

commit v1 on v0

--- a/solution.py
+++ b/solution.py
@@ -374,7 +374,7 @@
     total = 2 * rows + SPAN_PAD
     return pl.pallas_call(
         functools.partial(kernel, n, width ** (-0.5)),
-        out_shape=jax.ShapeDtypeStruct((1, H * width), bf16),
+        out_shape=pltpu.VMEM((1, H * width), bf16),
         in_specs=[pl.BlockSpec(memory_space=pltpu.HBM)] * 9,
         out_specs=pl.BlockSpec(memory_space=pltpu.VMEM),
         scratch_shapes=[

time: 20.8 us -> 19.4 us (0.933)
  local copies, waits for them, and re-layouts: 1.41 us -> 0.62 us
  Pallas kernels: 17.9 us -> 17.3 us
    unnamed x1, local copies, waits for them, and re-layouts: 1.41 us -> 0.62 us
    pallas_call x1, Pallas kernels: 17.9 us -> 17.3 us  [body(): pl.pallas_call(functools.partial(kernel, n, width ** (-0.5)), out_shape=p...]
where the time goes in v1:
time: 19.4 us; the launch traced here: 19.2 us
  Pallas kernels  17.3 us (89%)
  between operations  1.3 us (7%)
  local copies, waits for them, and re-layouts  0.62 us (3%)
    pallas_call x1, Pallas kernels, body(): pl.pallas_call(functools.partial(kernel, n, width ** (-0.5)), out_shape=p...  17.3 us
    unnamed x1, local copies, waits for them, and re-layouts  0.62 us

profile of v1, /device:TPU:0, one launch (start us, length us, event | category | flops | bytes accessed | tf_op | source)
XLA Modules:
  0.0 19.2 jit_solution(765751563160384847)
XLA Ops:
  1.3 17.3 %shard_map.91 = bf16[1,8192]{1,0:T(2,128)(2,1)S(1)} custom-call(s32[16]{0:T(128)} %table_hbm.1, s32[1]{0:T(128)S(6)} %copy.12.counts_hbm, s32[1]{0:T(128)S(6)} %copy.13.start_hbm, bf16[1,8192]{1,0:T(2,128)(2,1)} %q_hbm.1, bf16[1,1024]{1,0:T(2,128)(2,1)} %sk_hbm.1, bf16[1,1024]{1,0:T(2,128)(2,1)} %sv_hbm.1, f32[8,128]{1,0:T(8,128)} %constant.2.clone.tab_hbm, ...), custom_call_target="tpu_custom_call" | custom-call | tf_op jit(solution)/shard_map/pallas_call | solution.py:375
  18.6 0.6 %copy.11 = bf16[1,8192]{1,0:T(2,128)(2,1)} copy(bf16[1,8192]{1,0:T(2,128)(2,1)S(1)} %shard_map.91) | data formatting | bytes 32768
